TPU v7x, 32 devices: a whole 2x2x4 slice. The times are simulated.
32 devices in a mesh: dp: 8 (over z, core), tensor: 4 (over y, x).
Axes of the slice: x: 2, y: 2, z: 4, core: 2. Of those that a mesh axis runs over, the one named last changes fastest.
Arguments:
- latents: bfloat16 [88, 256, 640], P('dp', 'tensor'), may hold values from -6 to 6
- cotangent: bfloat16 [88, 256, 640], P('dp', 'tensor'), may hold values from -6 to 6
- trunc_steps: int32 [8], replicated, may hold values from 30 to 40, as said below
- timesteps: int32 [88], replicated, may hold values from 100 to 900
- tile_map: int32 [88], replicated, may hold values from 0 to 87, as said below
- gain: float32 [640], replicated, may hold values from 0.5 to 1.5
- w_value: bfloat16 [640, 2560], P(None, 'tensor'), may hold values from -0.25 to 0.25
- w_gate: bfloat16 [640, 2560], P(None, 'tensor'), may hold values from -0.25 to 0.25
- w_out: bfloat16 [640, 2560], P(None, 'tensor'), may hold values from -0.125 to 0.125
Outputs:
- placed_grad: bfloat16 [88, 256, 640], P('dp', 'tensor')
- grad_value: float32 [640, 2560], P('dp', 'tensor')
- grad_gate: float32 [640, 2560], P('dp', 'tensor')
- grad_out_proj: float32 [640, 2560], P('dp', 'tensor')
- grad_gain: float32 [640], replicated
Inputs may be any that keep to these rules, and one draw needn't show every extreme that they name: trunc_steps lies in 30 to 40, so a prompt has 1 to 11 live slots, its lowest ones. tile_map is a permutation of 0 to 87. Output slots g * 11 to g * 11 + 10 form group g; the live items go to the lowest slots of the groups, and each group receives the floor or the ceiling of (number of live items) / 8 of them.
All inputs are finite; a program needn't handle non-finite values.
Results may differ from a plain program's by a relative error of at most 0.0068.
Values may be sent and summed in bfloat16 or wider, within the bound.
A program may use at most 64 MiB of HBM per device.

v0:
```python
import functools

import jax
import jax.numpy as jnp
import numpy as np
from jax import lax
from jax.experimental import pallas as pl
from jax.experimental.pallas import tpu as pltpu
from jax.sharding import PartitionSpec as P

eps = 1e-05


def noise_table():
    betas = np.linspace(0.00085**0.5, 0.012**0.5, 1000) ** 2
    abar = np.exp(np.cumsum(np.log1p(-betas)))
    return np.sqrt(1.0 - abar).astype(np.float32)


def block_kernel(n, groups, ahead, lag, late, scale_ref, source_ref, x_ref, cot_ref, gain_ref,
                 wv_ref, wg_ref, wo_ref, ig_ref, gg_ref, dv_ref, dg_ref, do_ref,
                 full, part, other, acc_v, acc_g, acc_o, placed, gain_one, gain_two,
                 dw_part, dw_pair, dw_sum, dw_other,
                 ag_send, ag_recv, rs_send, rs_recv, out_send, out_recv,
                 gain_send, gain_recv, far_send, far_recv,
                 pair_send, pair_recv, sum_send, sum_recv):
    slots, rows, width = x_ref.shape
    inner = wv_ref.shape[1]
    me = lax.axis_index("tensor")
    high = n // 2
    my_high, my_low = me // 2, me % 2
    pair = my_high * 2 + (1 - my_low)
    line = [((my_high + k) % high) * 2 + my_low for k in range(1, high)]
    peers = [(me + k) % n for k in range(1, n)]
    first = (((0,), (0,)), ((), ()))
    last = (((1,), (1,)), ((), ()))
    local = (x_ref, cot_ref)
    group = lax.axis_index("dp")
    chips = groups // 2
    chip, core = group // 2, group % 2
    twin = chip * 2 + (1 - core)
    away = [((chip + k) % chips) for k in range(1, chips)]
    block = dw_part.shape[1]

    def cross(src, dst, send_sem, recv_sem, peer):
        return pltpu.make_async_remote_copy(
            src_ref=src, dst_ref=dst, send_sem=send_sem, recv_sem=recv_sem,
            device_id={"dp": peer}, device_id_type=pl.DeviceIdType.MESH,
        )

    def out_copy(t, owner, index, peer):
        spot = placed.at[owner * slots + t]
        return cross(spot, spot, out_send.at[t, index], out_recv.at[t, owner], peer)

    def out_own(t):
        found = [out_copy(t, group, k, c * 2 + core) for k, c in enumerate(away)]
        return found + [out_copy(t, group, chips - 1, twin)]

    def out_passed(t):
        return [out_copy(t, c * 2 + core, chips + k, twin) for k, c in enumerate(away)]

    def pass_out(t):
        for c, copy in zip(away, out_passed(t), strict=True):
            out_copy(t, c * 2 + core, 0, twin).wait_recv()
            copy.start()

    def send(src, dst, send_sem, recv_sem, peer):
        return pltpu.make_async_remote_copy(
            src_ref=src, dst_ref=dst, send_sem=send_sem, recv_sem=recv_sem,
            device_id={"tensor": peer}, device_id_type=pl.DeviceIdType.MESH,
        )

    def own_copies(t):
        found = []
        for peer in [pair] + line:
            for kind in (0, 1):
                found.append(send(
                    local[kind].at[t], full.at[t, kind, me],
                    ag_send.at[t, len(found)], ag_recv.at[t, kind, me], peer,
                ))
        return found

    def passed_copies(t):
        found = []
        base = 2 * high
        for peer in line:
            found.append(send(
                full.at[t, 0, pair], full.at[t, 0, pair],
                ag_send.at[t, base + len(found)], ag_recv.at[t, 0, pair], peer,
            ))
        for owner in line:
            found.append(send(
                full.at[t, 1, owner], full.at[t, 1, owner],
                ag_send.at[t, base + len(found)], ag_recv.at[t, 1, owner], pair,
            ))
        return found

    def arrived(t, kind, owner):
        send(full.at[t, kind, owner], full.at[t, kind, owner], ag_send.at[t, 0],
             ag_recv.at[t, kind, owner], pair).wait_recv()

    def sum_copies(t):
        return [
            send(part.at[t, peer], other.at[t, me], rs_send.at[t, k], rs_recv.at[t, me], peer)
            for k, peer in enumerate(peers)
        ]

    def start_own(t):
        for copy in own_copies(t):
            copy.start()

    def pass_on(t):
        for owner in [pair] + line:
            for kind in (0, 1):
                arrived(t, kind, owner)
        for copy in passed_copies(t):
            copy.start()

    barrier = pltpu.get_barrier_semaphore()
    for peer in peers:
        pl.semaphore_signal(
            barrier, inc=1, device_id={"tensor": peer}, device_id_type=pl.DeviceIdType.MESH
        )
    for k in range(1, groups):
        pl.semaphore_signal(
            barrier, inc=1, device_id={"dp": (group + k) % groups},
            device_id_type=pl.DeviceIdType.MESH,
        )
    pl.semaphore_wait(barrier, n - 1 + groups - 1)
    for t in range(ahead):
        start_own(t)
    acc_v[...] = jnp.zeros_like(acc_v)
    acc_g[...] = jnp.zeros_like(acc_g)
    acc_o[...] = jnp.zeros_like(acc_o)
    gg_ref[...] = jnp.zeros_like(gg_ref)
    pass_on(0)

    def finish(t):
        d_normed = part[t, me].astype(jnp.float32)
        for peer in peers:
            send(part.at[t, peer], other.at[t, peer], rs_send.at[t, 0], rs_recv.at[t, peer],
                 peer).wait_recv()
            d_normed += other[t, peer].astype(jnp.float32)
        x = x_ref[t].astype(jnp.float32)
        centred = x - jnp.mean(x, axis=-1, keepdims=True)
        inv_std = lax.rsqrt(jnp.mean(centred * centred, axis=-1, keepdims=True) + eps)
        x_hat = centred * inv_std
        grad = (cot_ref[t].astype(jnp.float32) * scale_ref[t]).astype(jnp.bfloat16)
        d_hat = d_normed * gain_ref[...]
        placed[group * slots + t] = (grad.astype(jnp.float32) + inv_std * (
            d_hat
            - jnp.mean(d_hat, axis=-1, keepdims=True)
            - x_hat * jnp.mean(d_hat * x_hat, axis=-1, keepdims=True)
        )).astype(jnp.bfloat16)
        for copy in out_own(t):
            copy.start()
        gg_ref[...] += jnp.sum(d_normed * x_hat, axis=0, keepdims=True)

    def one_tile(t, carry):
        @pl.when(t + ahead < slots)
        def _():
            start_own(t + ahead)

        @pl.when(t + 1 < slots)
        def _():
            pass_on(t + 1)

        full[t, 0, me] = x_ref[t]
        full[t, 1, me] = cot_ref[t]
        far = [((my_high + k) % high) * 2 + (1 - my_low) for k in range(1, high)]
        for owner in far:
            for kind in (0, 1):
                arrived(t, kind, owner)
        x = full[t, 0].reshape(n * rows, width).astype(jnp.float32)
        centred = x - jnp.mean(x, axis=-1, keepdims=True)
        inv_std = lax.rsqrt(jnp.mean(centred * centred, axis=-1, keepdims=True) + eps)
        normed = (centred * inv_std * gain_ref[...]).astype(jnp.bfloat16)
        cot = full[t, 1].reshape(n * rows, width).astype(jnp.float32)
        grad = (cot * scale_ref[t]).astype(jnp.bfloat16)
        values = jnp.dot(normed, wv_ref[...], preferred_element_type=jnp.float32)
        gate = jnp.dot(normed, wg_ref[...], preferred_element_type=jnp.float32)
        d_hidden = jnp.dot(grad, wo_ref[...], preferred_element_type=jnp.float32)
        cdf = 0.5 * (1.0 + lax.erf(gate * 0.7071067811865476))
        density = jnp.exp(-0.5 * gate * gate) * 0.3989422804014327
        gelu = gate * cdf
        hidden = (values * gelu).astype(jnp.bfloat16)
        d_value = (d_hidden * gelu).astype(jnp.bfloat16)
        d_gate = (d_hidden * values * (cdf + gate * density)).astype(jnp.bfloat16)
        d_normed = lax.dot_general(d_value, wv_ref[...], last, preferred_element_type=jnp.float32)
        d_normed += lax.dot_general(d_gate, wg_ref[...], last, preferred_element_type=jnp.float32)
        part[t] = d_normed.astype(jnp.bfloat16).reshape(n, rows, width)
        for copy in sum_copies(t):
            copy.start()
        acc_v[...] += lax.dot_general(normed, d_value, first, preferred_element_type=jnp.float32)
        acc_g[...] += lax.dot_general(normed, d_gate, first, preferred_element_type=jnp.float32)
        acc_o[...] += lax.dot_general(grad, hidden, first, preferred_element_type=jnp.float32)

        @pl.when(t >= lag)
        def _():
            finish(t - lag)

        @pl.when(t >= lag + late)
        def _():
            pass_out(t - lag - late)

        return carry

    lax.fori_loop(0, slots, one_tile, 0)
    for d in range(groups):
        rows_of = slice(d * block, (d + 1) * block)
        for k, acc in enumerate((acc_v, acc_g, acc_o)):
            dw_part[d, :, k * inner : (k + 1) * inner] = acc[rows_of, :].astype(jnp.bfloat16)
    pair_copies = [
        cross(dw_part.at[c * 2 + 1 - core], dw_pair.at[c], pair_send.at[c], pair_recv.at[c], twin)
        for c in range(chips)
    ]
    for copy in pair_copies:
        copy.start()

    def drain(t, carry):
        finish(t)
        return carry

    lax.fori_loop(slots - lag, slots, drain, 0)
    gain_one[me] = gg_ref[...]
    gain_copies = [
        send(gg_ref, gain_one.at[me], gain_send.at[k], gain_recv.at[me], peer)
        for k, peer in enumerate(peers)
    ]
    for copy in gain_copies:
        copy.start()
    for copy in pair_copies:
        copy.wait()
    for c in range(chips):
        both = dw_part[c * 2 + core].astype(jnp.float32) + dw_pair[c].astype(jnp.float32)
        dw_sum[c] = both.astype(jnp.bfloat16)
    sum_copies_z = [
        cross(dw_sum.at[c], dw_other.at[chip], sum_send.at[k], sum_recv.at[chip], c * 2 + core)
        for k, c in enumerate(away)
    ]
    for copy in sum_copies_z:
        copy.start()

    def drain_out(t, carry):
        pass_out(t)
        return carry

    lax.fori_loop(slots - lag - late, slots, drain_out, 0)
    for peer in peers:
        send(gg_ref, gain_one.at[peer], gain_send.at[0], gain_recv.at[peer], peer).wait_recv()
    for copy in gain_copies:
        copy.wait_send()
    gain_sum = gain_one[0]
    for k in range(1, n):
        gain_sum += gain_one[k]
    gain_two[group] = gain_sum
    far_copies = [
        cross(gain_two.at[group], gain_two.at[group], far_send.at[k], far_recv.at[group],
              (group + k) % groups)
        for k in range(1, groups)
    ]
    for copy in far_copies:
        copy.start()

    def settle(t, carry):
        for c in range(chips):
            out_copy(t, c * 2 + 1 - core, 0, twin).wait_recv()
        for copy in own_copies(t) + passed_copies(t) + sum_copies(t) + out_own(t) + out_passed(t):
            copy.wait_send()
        return carry

    lax.fori_loop(0, slots, settle, 0)

    def place(t, carry):
        ig_ref[t] = placed[source_ref[t]]
        return carry

    lax.fori_loop(0, slots, place, 0)
    for k in range(1, groups):
        peer = (group + k) % groups
        cross(gain_two.at[peer], gain_two.at[peer], far_send.at[k], far_recv.at[peer],
              peer).wait_recv()
    for copy in far_copies:
        copy.wait_send()
    gain_total = gain_two[0]
    for k in range(1, groups):
        gain_total += gain_two[k]
    gg_ref[...] = gain_total
    result = dw_sum[chip].astype(jnp.float32)
    for c in away:
        cross(dw_other.at[c], dw_other.at[c], sum_send.at[0], sum_recv.at[c], twin).wait_recv()
        result += dw_other[c].astype(jnp.float32)
    for copy in sum_copies_z:
        copy.wait_send()
    dv_ref[...] = result[:, 0:inner]
    dg_ref[...] = result[:, inner : 2 * inner]
    do_ref[...] = result[:, 2 * inner : 3 * inner]


def block_backward(n, groups, scale, source, x, cot, gain, w_value, w_gate, w_out):
    slots, rows, width = x.shape
    inner = w_value.shape[1]
    chips = groups // 2
    block = width // groups
    vmem = pl.BlockSpec(memory_space=pltpu.VMEM)
    smem = pl.BlockSpec(memory_space=pltpu.SMEM)
    grads = jax.ShapeDtypeStruct((block, inner), jnp.float32)
    dma = pltpu.SemaphoreType.DMA
    return pl.pallas_call(
        functools.partial(block_kernel, n, groups, 3, 2, 2),
        in_specs=[smem] * 2 + [vmem] * 6,
        out_specs=[vmem] * 5,
        out_shape=[
            jax.ShapeDtypeStruct((slots, rows, width), jnp.bfloat16),
            jax.ShapeDtypeStruct((1, width), jnp.float32),
            grads,
            grads,
            grads,
        ],
        scratch_shapes=[
            pltpu.VMEM((slots, 2, n, rows, width), jnp.bfloat16),
            pltpu.VMEM((slots, n, rows, width), jnp.bfloat16),
            pltpu.VMEM((slots, n, rows, width), jnp.bfloat16),
        ]
        + [pltpu.VMEM((width, inner), jnp.float32)] * 3
        + [
            pltpu.VMEM((groups * slots, rows, width), jnp.bfloat16),
            pltpu.VMEM((n, 1, width), jnp.float32),
            pltpu.VMEM((groups, 1, width), jnp.float32),
            pltpu.VMEM((groups, block, 3 * inner), jnp.bfloat16),
            pltpu.VMEM((chips, block, 3 * inner), jnp.bfloat16),
            pltpu.VMEM((chips, block, 3 * inner), jnp.bfloat16),
            pltpu.VMEM((chips, block, 3 * inner), jnp.bfloat16),
            dma((slots, n + 2 * (n // 2 - 1))),
            dma((slots, 2, n)),
            dma((slots, n)),
            dma((slots, n)),
            dma((slots, 2 * chips - 1)),
            dma((slots, groups)),
            dma((n,)),
            dma((n,)),
            dma((groups,)),
            dma((groups,)),
            dma((chips,)),
            dma((chips,)),
            dma((chips,)),
            dma((chips,)),
        ],
        compiler_params=pltpu.CompilerParams(
            collective_id=0, has_side_effects=True, vmem_limit_bytes=60 * 1024 * 1024
        ),
    )(scale, source, x, cot, gain, w_value, w_gate, w_out)


def per_device(latents, cotangent, trunc_steps, timesteps, tile_map, gain, w_value, w_gate, w_out):
    slots, local_rows, width = latents.shape
    total = tile_map.shape[0]
    inner = w_value.shape[1]
    me = lax.axis_index("dp")
    live = jnp.clip(lax.dynamic_index_in_dim(trunc_steps, me, 0, keepdims=True) - 29, 1, slots)
    times = lax.dynamic_slice_in_dim(timesteps, me * slots, slots, 0)
    table = jnp.asarray(noise_table())
    scale = jnp.sum(
        jnp.where(times[:, None] == jnp.arange(1000, dtype=jnp.int32)[None, :], table[None, :], 0.0),
        axis=1,
    )
    scale = jnp.where(jnp.arange(slots, dtype=jnp.int32) < live[0], scale, 0.0)
    item_ids = jnp.arange(total, dtype=jnp.int32)
    my_slots = me * slots + jnp.arange(slots, dtype=jnp.int32)
    source = jnp.sum(
        jnp.where(tile_map[:, None] == my_slots[None, :], item_ids[:, None], 0), axis=0
    )
    placed, grad_gain, grad_value, grad_gate, grad_out_proj = block_backward(
        lax.axis_size("tensor"), lax.axis_size("dp"), scale, source, latents, cotangent,
        gain[None, :], w_value, w_gate, w_out,
    )
    return (placed, grad_value, grad_gate, grad_out_proj, grad_gain[0])


def solution(mesh):
    in_specs = (
        P("dp", "tensor", None),
        P("dp", "tensor", None),
        P(),
        P(),
        P(),
        P(),
        P(None, "tensor"),
        P(None, "tensor"),
        P(None, "tensor"),
    )
    out_specs = (
        P("dp", "tensor", None),
        P("dp", "tensor"),
        P("dp", "tensor"),
        P("dp", "tensor"),
        P(),
    )
    return jax.shard_map(
        per_device, mesh=mesh, in_specs=in_specs, out_specs=out_specs, check_vma=False
    )
```

profile of v0, /device:TPU:12, one launch (start us, length us, event | category | flops | bytes accessed | tf_op | source)
XLA Modules:
  0.0 169.0 jit_solution(4000746859027358158)
XLA Ops:
  0.6 0.0 copy-start.6
  0.7 0.6 copy-done.6
  1.3 0.0 copy-start.7
  1.3 0.7 select_reduce_fusion.1.source_ref
  2.0 0.0 copy-done.7
  2.0 0.0 copy-start.8
  2.0 0.1 dynamic_slice.8
  2.1 0.6 copy-done.8
  2.6 0.6 dynamic_slice.7
  3.2 0.0 copy-start.3
  3.9 0.0 copy-start.4
  3.9 0.0 copy-done.3
  3.9 0.2 select_reduce_fusion
  4.1 0.5 compare_select_fusion.scale_ref
  4.6 0.0 copy-done.4
  4.6 0.6 broadcast_in_dim.42.gain_ref
  5.2 157.6 %shard_map.137 = (bf16[11,64,640]{2,1,0:T(8,128)(2,1)}, f32[1,640]{1,0:T(1,128)}, f32[80,640]{1,0:T(8,128)}, f32[80,640]{1,0:T(8,128)}, f32[80,640]{1,0:T(8,128)}) custom-call(f32[11]{0:T(128)} %compare_select_fusion.scale_ref, s32[11]{0:T(128)} %select_reduce_fusion.1.source_ref, bf16[11,64,640]{2,1,0:T(8,128)(2,1)} %x_ref.1, bf16[11,64,640]{2,1,0:T(8,128)(2,1)} %cot_ref.1, ...), custom_call_target="tpu_custom_call" | custom-call | tf_op jit(solution)/shard_map/pallas_call | solution.py:309
  162.8 0.0 copy-start.5
  162.9 0.7 copy-done.5
  163.5 0.6 reduce
  164.1 0.0 copy-start.2
  164.1 2.2 %copy.19 = bf16[11,64,640]{2,1,0:T(8,128)(2,1)} copy(bf16[11,64,640]{2,1,0:T(8,128)(2,1)} %get-tuple-element.20) | data formatting | bytes 1802240
  166.3 0.0 copy-done.2
  166.3 0.0 copy-start.1
  166.3 0.7 copy.20
  167.0 0.3 copy-done.1
  167.3 0.0 copy-start
  167.3 0.7 copy.21
  168.0 0.3 copy-done
  168.3 0.7 copy.22
  (1 shorter events, 0.0 us)
Async XLA Ops:
  0.6 0.7 copy-start.6
  1.3 0.7 copy-start.7
  2.0 0.7 copy-start.8
  3.2 0.7 copy-start.3
  3.9 0.7 copy-start.4
  162.8 0.7 copy-start.5
  164.1 2.2 %copy-start.2 = (f32[80,640]{1,0:T(8,128)S(1)}, f32[80,640]{1,0:T(8,128)}, u32[]{:S(2)}) copy-start(f32[80,640]{1,0:T(8,128)} %get-tuple-element.21) | copy-start | bytes 614404
  166.3 1.0 copy-start.1
  167.3 1.0 copy-start
where the time goes:
time: 172 us; the launch traced here: 169 us
  Pallas kernels  158 us (92%)
  local copies, waits for them, and re-layouts  8.03 us (5%)
  other arithmetic  2.01 us (1%)
    pallas_call x1, Pallas kernels, block_backward(): pl.pallas_call(functools.partial(block_kernel, n, groups, 3, 2, 2), in_sp...  158 us
    unnamed x22, local copies, waits for them, and re-layouts  6.79 us

commit v1 on v0

v1 whole, which is shorter than its diff:
```python
import functools

import jax
import jax.numpy as jnp
import numpy as np
from jax import lax
from jax.experimental import pallas as pl
from jax.experimental.pallas import tpu as pltpu
from jax.sharding import PartitionSpec as P

eps = 1e-05


def noise_table():
    betas = np.linspace(0.00085**0.5, 0.012**0.5, 1000) ** 2
    abar = np.exp(np.cumsum(np.log1p(-betas)))
    return np.sqrt(1.0 - abar).astype(np.float32)


def block_kernel(n, groups, rounds, ahead, steps_ref, times_ref, map_ref, table_ref, x_ref, cot_ref,
                 gain_ref, wv_ref, wg_ref, wo_ref, ig_ref, gg_ref, dv_ref, dg_ref, do_ref,
                 full, part_a, part_b, in_a, in_b, sum_a, sum_b, last_a, last_b, held,
                 acc_v, acc_g, acc_o, placed, gain_one, gain_two,
                 dw_part, dw_pair, dw_sum, dw_down, dw_up, pool, scale_ref, source_ref, keep_ref,
                 ag_send, ag_recv, sa_send, sa_recv, sb_send, sb_recv, ta_send, ta_recv,
                 tb_send, tb_recv, out_send, out_recv, gain_send, gain_recv, far_send, far_recv,
                 pair_send, pair_recv, down_send, down_recv, up_send, up_recv,
                 pool_send, pool_recv):
    slots, rows, width = x_ref.shape
    half = rows // 2
    extra = slots - rounds
    me = lax.axis_index("tensor")
    high = n // 2
    my_high, my_low = me // 2, me % 2
    pair = my_high * 2 + (1 - my_low)
    line_high = [(my_high + k) % high for k in range(1, high)]
    line = [h * 2 + my_low for h in line_high]
    peers = [(me + k) % n for k in range(1, n)]
    first = (((0,), (0,)), ((), ()))
    last = (((1,), (1,)), ((), ()))
    group = lax.axis_index("dp")
    chips = groups // 2
    chip, core = group // 2, group % 2
    twin = chip * 2 + (1 - core)
    block = dw_part.shape[2]
    own_live = jnp.clip(steps_ref[group] - 29, 1, slots)
    twin_live = jnp.clip(steps_ref[twin] - 29, 1, slots)

    def cross(src, dst, send_sem, recv_sem, peer):
        return pltpu.make_async_remote_copy(
            src_ref=src, dst_ref=dst, send_sem=send_sem, recv_sem=recv_sem,
            device_id={"dp": peer}, device_id_type=pl.DeviceIdType.MESH,
        )

    def send(src, dst, send_sem, recv_sem, peer):
        return pltpu.make_async_remote_copy(
            src_ref=src, dst_ref=dst, send_sem=send_sem, recv_sem=recv_sem,
            device_id={"tensor": peer}, device_id_type=pl.DeviceIdType.MESH,
        )

    def out_copy(t, owner, index, peer):
        spot = placed.at[owner * rounds + t]
        return cross(spot, spot, out_send.at[t, index], out_recv.at[t, owner], peer)

    def own_outs(t, act):
        @pl.when(chip + 1 < chips)
        def _():
            act(out_copy(t, group, 0, group + 2))

        @pl.when(chip >= 1)
        def _():
            act(out_copy(t, group, 1, group - 2))

        act(out_copy(t, group, 2, twin))

    def relay_outs(t, d, act, arrive):
        base = 3 + 4 * (d - 1)

        @pl.when(chip >= d)
        def _():
            owner = group - 2 * d
            if arrive:
                out_copy(t, owner, base, twin).wait_recv()

            @pl.when(chip + 1 < chips)
            def _():
                act(out_copy(t, owner, base, group + 2))

            act(out_copy(t, owner, base + 1, twin))

        @pl.when(chip + d < chips)
        def _():
            owner = group + 2 * d
            if arrive:
                out_copy(t, owner, base + 2, twin).wait_recv()

            @pl.when(chip >= 1)
            def _():
                act(out_copy(t, owner, base + 2, group - 2))

            act(out_copy(t, owner, base + 3, twin))

    def begin(copy):
        copy.start()

    def done(copy):
        copy.wait_send()

    def own_copies(t):
        found = []
        for peer in [pair] + line:
            for kind in (0, 1):
                found.append(send(
                    full.at[t, kind, me], full.at[t, kind, me],
                    ag_send.at[t, len(found)], ag_recv.at[t, kind, me], peer,
                ))
        return found

    def passed_copies(t):
        found = []
        base = 2 * high
        for peer in line:
            found.append(send(
                full.at[t, 0, pair], full.at[t, 0, pair],
                ag_send.at[t, base + len(found)], ag_recv.at[t, 0, pair], peer,
            ))
        for owner in line:
            found.append(send(
                full.at[t, 1, owner], full.at[t, 1, owner],
                ag_send.at[t, base + len(found)], ag_recv.at[t, 1, owner], pair,
            ))
        return found

    def arrived(t, kind, owner):
        send(full.at[t, kind, owner], full.at[t, kind, owner], ag_send.at[t, 0],
             ag_recv.at[t, kind, owner], pair).wait_recv()

    def one_a(t):
        return [send(part_a.at[t, 1 - my_low], in_a.at[t], sa_send.at[t], sa_recv.at[t], pair)]

    def one_b(t):
        return [
            send(part_b.at[t, h], in_b.at[t, k], sb_send.at[t, k], sb_recv.at[t, k], p)
            for k, (h, p) in enumerate(zip(line_high, line, strict=True))
        ]

    def two_a(t):
        return [
            send(sum_a.at[t, k], last_a.at[t, k], ta_send.at[t, k], ta_recv.at[t, k], p)
            for k, p in enumerate(line)
        ]

    def two_b(t):
        return [send(sum_b.at[t], last_b.at[t], tb_send.at[t], tb_recv.at[t], pair)]

    def pick(values, index):
        found = values[0]
        for k in range(1, len(values)):
            found = jnp.where(index == k, values[k], found)
        return found

    def start_own(t):
        for copy in own_copies(t):
            copy.start()

    def pass_on(t):
        for owner in [pair] + line:
            for kind in (0, 1):
                arrived(t, kind, owner)
        for copy in passed_copies(t):
            copy.start()

    barrier = pltpu.get_barrier_semaphore()
    for peer in peers:
        pl.semaphore_signal(
            barrier, inc=1, device_id={"tensor": peer}, device_id_type=pl.DeviceIdType.MESH
        )
    for k in range(1, groups):
        pl.semaphore_signal(
            barrier, inc=1, device_id={"dp": (group + k) % groups},
            device_id_type=pl.DeviceIdType.MESH,
        )
    for kind, ref in enumerate((x_ref, cot_ref)):
        full[0, kind, me] = ref[0]
    pl.semaphore_wait(barrier, n - 1 + groups - 1)
    pool_copies = [
        cross(ref.at[pl.ds(rounds, extra)], pool.at[kind], pool_send.at[kind], pool_recv.at[kind],
              twin)
        for kind, ref in enumerate((x_ref, cot_ref)) if extra
    ]
    start_own(0)
    for copy in pool_copies:
        copy.start()
    for copy in pool_copies:
        copy.wait()

    def fill(t, carry):
        for kind, ref in enumerate((x_ref, cot_ref)):
            tile = ref[t]
            if extra:
                spare = pool[kind, jnp.clip(t - own_live, 0, extra - 1)]
                tile = jnp.where(t < own_live, tile, spare)
            full[t, kind, me] = tile
        return carry

    lax.fori_loop(1, rounds, fill, 0)
    for t in range(1, min(ahead, rounds)):
        start_own(t)

    def set_scale(t, carry):
        mine = t < own_live
        item = jnp.where(mine, group * slots + t, twin * slots + rounds + t - own_live)
        item = jnp.clip(item, 0, groups * slots - 1)
        alive = jnp.logical_or(mine, rounds + t - own_live < twin_live)
        scale_ref[t] = jnp.where(alive, table_ref[times_ref[item]], 0.0)
        return carry

    lax.fori_loop(0, rounds, set_scale, 0)

    def invert(i, found):
        spot = map_ref[i] - group * slots
        return tuple(jnp.where(spot == s, i, item) for s, item in enumerate(found))

    items = lax.fori_loop(0, groups * slots, invert, tuple(jnp.int32(0) for _ in range(slots)))
    for s, item in enumerate(items):
        owner = item // slots
        index = item % slots
        live = jnp.clip(steps_ref[owner] - 29, 1, slots)
        other = owner + 1 - 2 * (owner % 2)
        other_live = jnp.clip(steps_ref[other] - 29, 1, slots)
        spot = jnp.where(
            index < rounds, owner * rounds + index, other * rounds + other_live + index - rounds
        )
        source_ref[s] = jnp.clip(spot, 0, groups * rounds - 1)
        keep_ref[s] = jnp.where(index < live, 1.0, 0.0)

    acc_v[...] = jnp.zeros_like(acc_v)
    acc_g[...] = jnp.zeros_like(acc_g)
    acc_o[...] = jnp.zeros_like(acc_o)
    gg_ref[...] = jnp.zeros_like(gg_ref)
    gain = gain_ref[...].reshape(1, width)
    pass_on(0)

    def combine(t):
        for copy in one_a(t):
            copy.wait_recv()
        sums = []
        for h in range(high):
            mine = pick([part_a[t, l, h] for l in range(2)], my_low)
            sums.append(mine.astype(jnp.float32) + in_a[t, h].astype(jnp.float32))
        for k, h in enumerate(line_high):
            sum_a[t, k] = pick(sums, h).astype(jnp.bfloat16)
        for copy in two_a(t):
            copy.start()
        held[t, 0] = pick(sums, my_high)
        for copy in one_b(t):
            copy.wait_recv()
        sums = []
        for l in range(2):
            both = pick([part_b[t, h, l] for h in range(high)], my_high).astype(jnp.float32)
            for k in range(high - 1):
                both += in_b[t, k, l].astype(jnp.float32)
            sums.append(both)
        sum_b[t] = pick(sums, 1 - my_low).astype(jnp.bfloat16)
        for copy in two_b(t):
            copy.start()
        held[t, 1] = pick(sums, my_low)

    def finish(t):
        top = held[t, 0]
        low = held[t, 1]
        for k, copy in enumerate(two_a(t)):
            copy.wait_recv()
            top += last_a[t, k].astype(jnp.float32)
        for copy in two_b(t):
            copy.wait_recv()
        low += last_b[t].astype(jnp.float32)
        d_normed = jnp.concatenate([top, low], axis=0)
        x = full[t, 0, me].astype(jnp.float32)
        centred = x - jnp.mean(x, axis=-1, keepdims=True)
        inv_std = lax.rsqrt(jnp.mean(centred * centred, axis=-1, keepdims=True) + eps)
        x_hat = centred * inv_std
        grad = (full[t, 1, me].astype(jnp.float32) * scale_ref[t]).astype(jnp.bfloat16)
        d_hat = d_normed * gain
        placed[group * rounds + t] = (grad.astype(jnp.float32) + inv_std * (
            d_hat
            - jnp.mean(d_hat, axis=-1, keepdims=True)
            - x_hat * jnp.mean(d_hat * x_hat, axis=-1, keepdims=True)
        )).astype(jnp.bfloat16)
        own_outs(t, begin)
        gg_ref[...] += jnp.sum(d_normed * x_hat, axis=0, keepdims=True)

    def after(t):
        @pl.when(t >= 1)
        def _():
            combine(t - 1)

        @pl.when(t >= 2)
        def _():
            finish(t - 2)

        for d in range(1, chips):
            @pl.when(t >= 2 + d)
            def _():
                relay_outs(t - 2 - d, d, begin, True)

    def relay_left(t):
        for d in range(1, chips):
            if 0 <= t - 2 - d < rounds:
                relay_outs(t - 2 - d, d, begin, True)

    def one_tile(t, carry):
        @pl.when(t + ahead < rounds)
        def _():
            start_own(t + ahead)

        @pl.when(t + 1 < rounds)
        def _():
            pass_on(t + 1)

        far = [h * 2 + (1 - my_low) for h in line_high]
        for owner in far:
            for kind in (0, 1):
                arrived(t, kind, owner)
        x = full[t, 0].reshape(n * rows, width).astype(jnp.float32)
        centred = x - jnp.mean(x, axis=-1, keepdims=True)
        inv_std = lax.rsqrt(jnp.mean(centred * centred, axis=-1, keepdims=True) + eps)
        normed = (centred * inv_std * gain).astype(jnp.bfloat16)
        cot = full[t, 1].reshape(n * rows, width).astype(jnp.float32)
        grad = (cot * scale_ref[t]).astype(jnp.bfloat16)
        values = jnp.dot(normed, wv_ref[...], preferred_element_type=jnp.float32)
        gate = jnp.dot(normed, wg_ref[...], preferred_element_type=jnp.float32)
        d_hidden = jnp.dot(grad, wo_ref[...], preferred_element_type=jnp.float32)
        cdf = 0.5 * (1.0 + lax.erf(gate * 0.7071067811865476))
        density = jnp.exp(-0.5 * gate * gate) * 0.3989422804014327
        gelu = gate * cdf
        hidden = (values * gelu).astype(jnp.bfloat16)
        d_value = (d_hidden * gelu).astype(jnp.bfloat16)
        d_gate = (d_hidden * values * (cdf + gate * density)).astype(jnp.bfloat16)
        d_normed = lax.dot_general(d_value, wv_ref[...], last, preferred_element_type=jnp.float32)
        d_normed += lax.dot_general(d_gate, wg_ref[...], last, preferred_element_type=jnp.float32)
        d_normed = d_normed.astype(jnp.bfloat16).reshape(n, rows, width)
        for h in range(high):
            for l in range(2):
                part_a[t, l, h] = d_normed[h * 2 + l, :half]
                part_b[t, h, l] = d_normed[h * 2 + l, half:]
        for copy in one_a(t) + one_b(t):
            copy.start()
        acc_v[...] += lax.dot_general(normed, d_value, first, preferred_element_type=jnp.float32)
        acc_g[...] += lax.dot_general(normed, d_gate, first, preferred_element_type=jnp.float32)
        acc_o[...] += lax.dot_general(grad, hidden, first, preferred_element_type=jnp.float32)
        after(t)
        return carry

    lax.fori_loop(0, rounds, one_tile, 0)
    for d in range(groups):
        rows_of = slice(d * block, (d + 1) * block)
        for k, acc in enumerate((acc_v, acc_g, acc_o)):
            dw_part[d, k] = acc[rows_of, :].astype(jnp.bfloat16)
    pair_copies = [
        cross(dw_part.at[c * 2 + 1 - core], dw_pair.at[c], pair_send.at[c], pair_recv.at[c], twin)
        for c in range(chips)
    ]
    for copy in pair_copies:
        copy.start()

    combine(rounds - 1)
    for t in (rounds, rounds + 1):
        if t >= 2:
            finish(t - 2)
        relay_left(t)
    gain_one[me] = gg_ref[...]
    gain_copies = [
        send(gg_ref, gain_one.at[me], gain_send.at[k], gain_recv.at[me], peer)
        for k, peer in enumerate(peers)
    ]
    for copy in gain_copies:
        copy.start()
    for copy in pair_copies:
        copy.wait()
    for c in range(chips):
        both = dw_part[c * 2 + core].astype(jnp.float32) + dw_pair[c].astype(jnp.float32)
        dw_sum[c] = both.astype(jnp.bfloat16)

    def down_copy(c, k):
        return cross(dw_sum.at[c, k], dw_down.at[c, k], down_send.at[c, k], down_recv.at[c, k],
                     group - 2)

    def up_copy(c, k):
        return cross(dw_sum.at[c, k], dw_up.at[c, k], up_send.at[c, k], up_recv.at[c, k], group + 2)

    def move(j, k):
        @pl.when(chip > j)
        def _():
            @pl.when(chip + 1 < chips)
            def _():
                down_copy(j, k).wait_recv()
                both = dw_sum[j, k].astype(jnp.float32) + dw_down[j, k].astype(jnp.float32)
                dw_sum[j, k] = both.astype(jnp.bfloat16)

            down_copy(j, k).start()

        c = chips - 1 - j

        @pl.when(chip < c)
        def _():
            @pl.when(chip >= 1)
            def _():
                up_copy(c, k).wait_recv()
                both = dw_sum[c, k].astype(jnp.float32) + dw_up[c, k].astype(jnp.float32)
                dw_sum[c, k] = both.astype(jnp.bfloat16)

            up_copy(c, k).start()

    for j in range(chips - 1):
        for k in range(3):
            move(j, k)
    for t in range(rounds + 2, rounds + 1 + chips):
        relay_left(t)
    for peer in peers:
        send(gg_ref, gain_one.at[peer], gain_send.at[0], gain_recv.at[peer], peer).wait_recv()
    for copy in gain_copies:
        copy.wait_send()
    gain_sum = gain_one[0]
    for k in range(1, n):
        gain_sum += gain_one[k]
    gain_two[group] = gain_sum
    far_copies = [
        cross(gain_two.at[group], gain_two.at[group], far_send.at[k], far_recv.at[group],
              (group + k) % groups)
        for k in range(1, groups)
    ]
    for copy in far_copies:
        copy.start()

    def settle(t, carry):
        for c in range(chips):
            out_copy(t, c * 2 + 1 - core, 0, twin).wait_recv()
        for copy in (own_copies(t) + passed_copies(t) + one_a(t) + one_b(t) + two_a(t) + two_b(t)):
            copy.wait_send()
        own_outs(t, done)
        for d in range(1, chips):
            relay_outs(t, d, done, False)
        return carry

    lax.fori_loop(0, rounds, settle, 0)

    def place(t, carry):
        ig_ref[t] = (placed[source_ref[t]].astype(jnp.float32) * keep_ref[t]).astype(jnp.bfloat16)
        return carry

    lax.fori_loop(0, slots, place, 0)
    for k in range(1, groups):
        peer = (group + k) % groups
        cross(gain_two.at[peer], gain_two.at[peer], far_send.at[k], far_recv.at[peer],
              peer).wait_recv()
    for copy in far_copies:
        copy.wait_send()
    gain_total = gain_two[0]
    for k in range(1, groups):
        gain_total += gain_two[k]
    gg_ref[...] = gain_total
    outs = (dv_ref, dg_ref, do_ref)
    for c in range(chips):
        @pl.when(chip == c)
        def _():
            for k, ref in enumerate(outs):
                total = dw_sum[c, k].astype(jnp.float32)
                if c + 1 < chips:
                    down_copy(c, k).wait_recv()
                    total += dw_down[c, k].astype(jnp.float32)
                if c >= 1:
                    up_copy(c, k).wait_recv()
                    total += dw_up[c, k].astype(jnp.float32)
                ref[...] = total

    for j in range(chips - 1):
        for k in range(3):
            @pl.when(chip > j)
            def _():
                down_copy(j, k).wait_send()

            @pl.when(chip < chips - 1 - j)
            def _():
                up_copy(chips - 1 - j, k).wait_send()


def block_backward(n, groups, rounds, ident, steps, times, tile_map, table, x, cot, gain,
                   w_value, w_gate, w_out):
    slots, rows, width = x.shape
    inner = w_value.shape[1]
    chips = groups // 2
    high = n // 2
    half = rows // 2
    others = max(high - 1, 1)
    block = width // groups
    vmem = pl.BlockSpec(memory_space=pltpu.VMEM)
    smem = pl.BlockSpec(memory_space=pltpu.SMEM)
    grads = jax.ShapeDtypeStruct((block, inner), jnp.float32)
    dma = pltpu.SemaphoreType.DMA
    bf16 = jnp.bfloat16
    return pl.pallas_call(
        functools.partial(block_kernel, n, groups, rounds, 3),
        in_specs=[smem] * 4 + [vmem] * 6,
        out_specs=[vmem] * 5,
        out_shape=[
            jax.ShapeDtypeStruct((slots, rows, width), bf16),
            jax.ShapeDtypeStruct((1, width), jnp.float32),
            grads,
            grads,
            grads,
        ],
        scratch_shapes=[
            pltpu.VMEM((rounds, 2, n, rows, width), bf16),
            pltpu.VMEM((rounds, 2, high, half, width), bf16),
            pltpu.VMEM((rounds, high, 2, half, width), bf16),
            pltpu.VMEM((rounds, high, half, width), bf16),
            pltpu.VMEM((rounds, others, 2, half, width), bf16),
            pltpu.VMEM((rounds, others, half, width), bf16),
            pltpu.VMEM((rounds, half, width), bf16),
            pltpu.VMEM((rounds, others, half, width), bf16),
            pltpu.VMEM((rounds, half, width), bf16),
            pltpu.VMEM((rounds, 2, half, width), jnp.float32),
        ]
        + [pltpu.VMEM((width, inner), jnp.float32)] * 3
        + [
            pltpu.VMEM((groups * rounds, rows, width), bf16),
            pltpu.VMEM((n, 1, width), jnp.float32),
            pltpu.VMEM((groups, 1, width), jnp.float32),
            pltpu.VMEM((groups, 3, block, inner), bf16),
            pltpu.VMEM((chips, 3, block, inner), bf16),
            pltpu.VMEM((chips, 3, block, inner), bf16),
            pltpu.VMEM((chips, 3, block, inner), bf16),
            pltpu.VMEM((chips, 3, block, inner), bf16),
            pltpu.VMEM((2, max(slots - rounds, 1), rows, width), bf16),
            pltpu.SMEM((rounds,), jnp.float32),
            pltpu.SMEM((slots,), jnp.int32),
            pltpu.SMEM((slots,), jnp.float32),
            dma((rounds, n + 2 * (high - 1))),
            dma((rounds, 2, n)),
            dma((rounds,)),
            dma((rounds,)),
            dma((rounds, high)),
            dma((rounds, high)),
            dma((rounds, high)),
            dma((rounds, high)),
            dma((rounds,)),
            dma((rounds,)),
            dma((rounds, 3 + 4 * (chips - 1))),
            dma((rounds, groups)),
            dma((n,)),
            dma((n,)),
            dma((groups,)),
            dma((groups,)),
            dma((chips,)),
            dma((chips,)),
            dma((chips, 3)),
            dma((chips, 3)),
            dma((chips, 3)),
            dma((chips, 3)),
            dma((2,)),
            dma((2,)),
        ],
        compiler_params=pltpu.CompilerParams(
            collective_id=ident, has_side_effects=True, vmem_limit_bytes=60 * 1024 * 1024
        ),
    )(steps, times, tile_map, table, x, cot, gain, w_value, w_gate, w_out)


def emit_kernel(ig_ref, gg_ref, dv_ref, dg_ref, do_ref, a_ref, b_ref, c_ref, d_ref, e_ref):
    a_ref[...] = ig_ref[...]
    b_ref[...] = dv_ref[...]
    c_ref[...] = dg_ref[...]
    d_ref[...] = do_ref[...]
    e_ref[...] = gg_ref[0, :]


def emit(ig, gg, dv, dg, do):
    vmem = pl.BlockSpec(memory_space=pltpu.VMEM)
    outs = [jax.ShapeDtypeStruct(a.shape, a.dtype) for a in (ig, dv, dg, do)]
    outs.append(jax.ShapeDtypeStruct((gg.shape[1],), gg.dtype))
    return pl.pallas_call(
        emit_kernel, in_specs=[vmem] * 5, out_specs=[vmem] * 5, out_shape=outs,
    )(ig, gg, dv, dg, do)


def per_device(latents, cotangent, trunc_steps, timesteps, tile_map, gain, w_value, w_gate, w_out):
    slots = latents.shape[0]
    n, groups = lax.axis_size("tensor"), lax.axis_size("dp")
    table = jnp.asarray(noise_table())
    args = (trunc_steps, timesteps, tile_map, table, latents, cotangent, gain, w_value, w_gate, w_out)
    results = block_backward(n, groups, slots, 0, *args)
    return tuple(emit(*results))


def solution(mesh):
    in_specs = (
        P("dp", "tensor", None),
        P("dp", "tensor", None),
        P(),
        P(),
        P(),
        P(),
        P(None, "tensor"),
        P(None, "tensor"),
        P(None, "tensor"),
    )
    out_specs = (
        P("dp", "tensor", None),
        P("dp", "tensor"),
        P("dp", "tensor"),
        P("dp", "tensor"),
        P(),
    )
    return jax.shard_map(
        per_device, mesh=mesh, in_specs=in_specs, out_specs=out_specs, check_vma=False
    )
```

time: 172 us -> 159 us (0.924); the launches traced: 169 us -> 158 us
  local copies, waits for them, and re-layouts: 8.03 us -> 0 us
  other arithmetic: 2.01 us -> 0 us
    unnamed x22 -> x0, local copies, waits for them, and re-layouts: 6.79 us -> none
    pallas_call x1 -> x2, Pallas kernels: 158 us -> 157 us  [the longest x1 155 us: block_backward(): pl.pallas_call(functools.partial(block_kernel, n, groups, rounds, 3), in_...]
where the time goes in v1:
time: 159 us; the launch traced here: 158 us
  Pallas kernels  157 us (99%)
    pallas_call x1, Pallas kernels, block_backward(): pl.pallas_call(functools.partial(block_kernel, n, groups, rounds, 3), in_...  155 us

profile of v1, /device:TPU:12, one launch (start us, length us, event | category | flops | bytes accessed | tf_op | source)
XLA Modules:
  0.0 157.9 jit_solution(17051507084291718026)
XLA Ops:
  0.6 154.7 %shard_map.137 = (bf16[11,64,640]{2,1,0:T(8,128)(2,1)}, f32[1,640]{1,0:T(1,128)}, f32[80,640]{1,0:T(8,128)}, f32[80,640]{1,0:T(8,128)}, f32[80,640]{1,0:T(8,128)}) custom-call(s32[8]{0:T(128)} %steps_ref.1, s32[88]{0:T(128)} %times_ref.1, s32[88]{0:T(128)} %map_ref.1, f32[1000]{0:T(1024)} %constant.2.clone.table_ref, bf16[11,64,640]{2,1,0:T(8,128)(2,1)} %x_ref.1, ...), custom_call_target="tpu_custom_call" | custom-call | tf_op jit(solution)/shard_map/pallas_call | solution.py:502
  155.4 2.5 %shard_map.138 = (bf16[11,64,640]{2,1,0:T(8,128)(2,1)}, f32[80,640]{1,0:T(8,128)}, f32[80,640]{1,0:T(8,128)}, f32[80,640]{1,0:T(8,128)}, f32[640]{0:T(1024)}) custom-call(bf16[11,64,640]{2,1,0:T(8,128)(2,1)} %get-tuple-element.10.ig_ref, f32[1,640]{1,0:T(1,128)} %get-tuple-element.11.gg_ref, f32[80,640]{1,0:T(8,128)} %get-tuple-element.12.dv_ref, ...), custom_call_target="tpu_custom_call" | custom-call | tf_op jit(solution)/shard_map/pallas_call | solution.py:582

commit v2 on v1

--- a/solution.py
+++ b/solution.py
@@ -9,6 +9,7 @@
 from jax.sharding import PartitionSpec as P
 
 eps = 1e-05
+early_round = 3
 
 
 def noise_table():
@@ -17,11 +18,35 @@
     return np.sqrt(1.0 - abar).astype(np.float32)
 
 
-def block_kernel(n, groups, rounds, ahead, steps_ref, times_ref, map_ref, table_ref, x_ref, cot_ref,
+def pick(values, index):
+    found = values[0]
+    for k in range(1, len(values)):
+        found = jnp.where(index == k, values[k], found)
+    return found
+
+
+def share(lives, rounds, early):
+    over = [jnp.maximum(live - rounds, 0) for live in lives]
+    near = [
+        jnp.minimum(over[q], jnp.maximum(rounds - lives[q ^ 1], 0)) for q in range(len(lives))
+    ]
+    spare = [over[q] - near[q] for q in range(len(lives))]
+    used = [jnp.minimum(live, rounds) + near[q ^ 1] for q, live in enumerate(lives)]
+    begin = [jnp.maximum(u, early) for u in used]
+    free = [rounds - b for b in begin]
+    spare_at, free_at = [jnp.int32(0)], [jnp.int32(0)]
+    for q in range(len(lives)):
+        spare_at.append(spare_at[q] + spare[q])
+        free_at.append(free_at[q] + free[q])
+    return near, used, begin, spare_at, free_at
+
+
+def block_kernel(n, groups, rounds, ahead, early, steps_ref, times_ref, map_ref, table_ref, x_ref, cot_ref,
                  gain_ref, wv_ref, wg_ref, wo_ref, ig_ref, gg_ref, dv_ref, dg_ref, do_ref,
                  full, part_a, part_b, in_a, in_b, sum_a, sum_b, last_a, last_b, held,
                  acc_v, acc_g, acc_o, placed, gain_one, gain_two,
-                 dw_part, dw_pair, dw_sum, dw_down, dw_up, pool, scale_ref, source_ref, keep_ref,
+                 dw_part, dw_pair, dw_sum, dw_down, dw_up, pool_near, pool_far, scale_ref, source_ref,
+                 keep_ref, from_ref, near_ref, far_ref, item_ref,
                  ag_send, ag_recv, sa_send, sa_recv, sb_send, sb_recv, ta_send, ta_recv,
                  tb_send, tb_recv, out_send, out_recv, gain_send, gain_recv, far_send, far_recv,
                  pair_send, pair_recv, down_send, down_recv, up_send, up_recv,
@@ -43,8 +68,15 @@
     chip, core = group // 2, group % 2
     twin = chip * 2 + (1 - core)
     block = dw_part.shape[2]
-    own_live = jnp.clip(steps_ref[group] - 29, 1, slots)
-    twin_live = jnp.clip(steps_ref[twin] - 29, 1, slots)
+    mate = group + 2 - 4 * (chip % 2)
+    base = group // 4 * 4
+    lives = [jnp.clip(steps_ref[base + q] - 29, 1, slots) for q in range(4)]
+    near, used, first_free, spare_at, free_at = share(lives, rounds, early)
+    seat = group % 4
+    own_live = pick(lives, seat)
+    own_used = pick(used, seat)
+    own_begin = pick(first_free, seat)
+    own_free_at = pick(free_at[:4], seat)
 
     def cross(src, dst, send_sem, recv_sem, peer):
         return pltpu.make_async_remote_copy(
@@ -153,12 +185,6 @@
     def two_b(t):
         return [send(sum_b.at[t], last_b.at[t], tb_send.at[t], tb_recv.at[t], pair)]
 
-    def pick(values, index):
-        found = values[0]
-        for k in range(1, len(values)):
-            found = jnp.where(index == k, values[k], found)
-        return found
-
     def start_own(t):
         for copy in own_copies(t):
             copy.start()
@@ -183,39 +209,69 @@
     for kind, ref in enumerate((x_ref, cot_ref)):
         full[0, kind, me] = ref[0]
     pl.semaphore_wait(barrier, n - 1 + groups - 1)
-    pool_copies = [
-        cross(ref.at[pl.ds(rounds, extra)], pool.at[kind], pool_send.at[kind], pool_recv.at[kind],
-              twin)
-        for kind, ref in enumerate((x_ref, cot_ref)) if extra
+    locals_ = (x_ref, cot_ref) if extra else ()
+    near_copies = [
+        cross(ref.at[pl.ds(rounds, extra)], pool_near.at[kind], pool_send.at[kind, 0],
+              pool_recv.at[kind, 0], twin)
+        for kind, ref in enumerate(locals_)
+    ]
+    far_pool = [
+        cross(ref.at[pl.ds(rounds, extra)], pool_far.at[kind, pl.ds(0, extra)],
+              pool_send.at[kind, 1], pool_recv.at[kind, 1], mate)
+        for kind, ref in enumerate(locals_)
+    ]
+    far_passed = [
+        cross(pool_far.at[kind, pl.ds(0, extra)], pool_far.at[kind, pl.ds(extra, extra)],
+              pool_send.at[kind, 2], pool_recv.at[kind, 2], twin)
+        for kind, ref in enumerate(locals_)
     ]
     start_own(0)
-    for copy in pool_copies:
+    for copy in near_copies + far_pool:
         copy.start()
-    for copy in pool_copies:
+
+    def set_scale(t, carry):
+        mine = t < own_live
+        beside = t < own_used
+        order = own_free_at + t - own_begin
+        item = base * slots
+        away_at = jnp.int32(0)
+        for q in range(4):
+            inside = jnp.logical_and(order >= spare_at[q], order < spare_at[q + 1])
+            k = near[q] + order - spare_at[q]
+            item = jnp.where(inside, (base + q) * slots + rounds + k, item)
+            away_at = jnp.where(inside, jnp.where(core == q % 2, 0, extra) + k, away_at)
+        item = jnp.where(beside, twin * slots + rounds + t - own_live, item)
+        item = jnp.where(mine, group * slots + t, item)
+        item = jnp.clip(item, 0, groups * slots - 1)
+        distant = jnp.logical_and(t >= own_begin, order < spare_at[4])
+        alive = jnp.logical_or(beside, distant)
+        scale_ref[t] = jnp.where(alive, table_ref[times_ref[item]], 0.0)
+        from_ref[t] = jnp.where(mine, 0, jnp.where(beside, 1, 2))
+        near_ref[t] = jnp.clip(t - own_live, 0, max(extra - 1, 0))
+        far_ref[t] = jnp.clip(away_at, 0, max(2 * extra - 1, 0))
+        return carry
+
+    lax.fori_loop(0, rounds, set_scale, 0)
+    for copy in near_copies:
         copy.wait()
 
     def fill(t, carry):
         for kind, ref in enumerate((x_ref, cot_ref)):
             tile = ref[t]
             if extra:
-                spare = pool[kind, jnp.clip(t - own_live, 0, extra - 1)]
-                tile = jnp.where(t < own_live, tile, spare)
+                tile = jnp.where(from_ref[t] == 0, tile, pool_near[kind, near_ref[t]])
             full[t, kind, me] = tile
         return carry
 
-    lax.fori_loop(1, rounds, fill, 0)
+    def fill_late(t, carry):
+        for kind, ref in enumerate((x_ref, cot_ref)):
+            tile = jnp.where(from_ref[t] == 0, ref[t], pool_near[kind, near_ref[t]])
+            full[t, kind, me] = jnp.where(from_ref[t] == 2, pool_far[kind, far_ref[t]], tile)
+        return carry
+
+    lax.fori_loop(1, early if extra else rounds, fill, 0)
     for t in range(1, min(ahead, rounds)):
         start_own(t)
-
-    def set_scale(t, carry):
-        mine = t < own_live
-        item = jnp.where(mine, group * slots + t, twin * slots + rounds + t - own_live)
-        item = jnp.clip(item, 0, groups * slots - 1)
-        alive = jnp.logical_or(mine, rounds + t - own_live < twin_live)
-        scale_ref[t] = jnp.where(alive, table_ref[times_ref[item]], 0.0)
-        return carry
-
-    lax.fori_loop(0, rounds, set_scale, 0)
 
     def invert(i, found):
         spot = map_ref[i] - group * slots
@@ -223,16 +279,33 @@
 
     items = lax.fori_loop(0, groups * slots, invert, tuple(jnp.int32(0) for _ in range(slots)))
     for s, item in enumerate(items):
+        item_ref[s] = item
+
+    def locate(s, carry):
+        item = item_ref[s]
         owner = item // slots
         index = item % slots
-        live = jnp.clip(steps_ref[owner] - 29, 1, slots)
+        root = owner // 4 * 4
+        place_in = owner - root
+        there = [jnp.clip(steps_ref[root + q] - 29, 1, slots) for q in range(4)]
+        near, used, first_free, spare_at, free_at = share(there, rounds, early)
         other = owner + 1 - 2 * (owner % 2)
-        other_live = jnp.clip(steps_ref[other] - 29, 1, slots)
-        spot = jnp.where(
-            index < rounds, owner * rounds + index, other * rounds + other_live + index - rounds
-        )
+        own_near = pick(near, place_in)
+        order = pick(spare_at[:4], place_in) + index - rounds - own_near
+        spot = jnp.int32(0)
+        for q in range(4):
+            inside = jnp.logical_and(order >= free_at[q], order < free_at[q + 1])
+            spot = jnp.where(
+                inside, (root + q) * rounds + first_free[q] + order - free_at[q], spot
+            )
+        beside = other * rounds + pick([there[q ^ 1] for q in range(4)], place_in) + index - rounds
+        spot = jnp.where(index < rounds + own_near, beside, spot)
+        spot = jnp.where(index < rounds, owner * rounds + index, spot)
         source_ref[s] = jnp.clip(spot, 0, groups * rounds - 1)
-        keep_ref[s] = jnp.where(index < live, 1.0, 0.0)
+        keep_ref[s] = jnp.where(index < pick(there, place_in), 1.0, 0.0)
+        return carry
+
+    lax.fori_loop(0, slots, locate, 0)
 
     acc_v[...] = jnp.zeros_like(acc_v)
     acc_g[...] = jnp.zeros_like(acc_g)
@@ -310,6 +383,13 @@
                 relay_outs(t - 2 - d, d, begin, True)
 
     def one_tile(t, carry):
+        if extra:
+            @pl.when(t == 1)
+            def _():
+                for copy in far_passed:
+                    copy.wait_recv()
+                lax.fori_loop(early, rounds, fill_late, 0)
+
         @pl.when(t + ahead < rounds)
         def _():
             start_own(t + ahead)
@@ -349,73 +429,90 @@
         acc_v[...] += lax.dot_general(normed, d_value, first, preferred_element_type=jnp.float32)
         acc_g[...] += lax.dot_general(normed, d_gate, first, preferred_element_type=jnp.float32)
         acc_o[...] += lax.dot_general(grad, hidden, first, preferred_element_type=jnp.float32)
+        if extra:
+            @pl.when(t == 0)
+            def _():
+                for copy in far_pool:
+                    copy.wait_recv()
+                for copy in far_passed:
+                    copy.start()
+
         after(t)
         return carry
 
     lax.fori_loop(0, rounds, one_tile, 0)
-    for d in range(groups):
-        rows_of = slice(d * block, (d + 1) * block)
-        for k, acc in enumerate((acc_v, acc_g, acc_o)):
-            dw_part[d, k] = acc[rows_of, :].astype(jnp.bfloat16)
     pair_copies = [
         cross(dw_part.at[c * 2 + 1 - core], dw_pair.at[c], pair_send.at[c], pair_recv.at[c], twin)
         for c in range(chips)
     ]
-    for copy in pair_copies:
-        copy.start()
-
+    ready = []
+    for j in range(chips - 1):
+        for c in (j, chips - 1 - j):
+            if c not in ready:
+                ready.append(c)
+                for d in (2 * c, 2 * c + 1):
+                    rows_of = slice(d * block, (d + 1) * block)
+                    for k, acc in enumerate((acc_v, acc_g, acc_o)):
+                        dw_part[d, k] = acc[rows_of, :].astype(jnp.bfloat16)
+                pair_copies[c].start()
     combine(rounds - 1)
-    for t in (rounds, rounds + 1):
-        if t >= 2:
-            finish(t - 2)
-        relay_left(t)
-    gain_one[me] = gg_ref[...]
+    if rounds >= 2:
+        finish(rounds - 2)
+    relay_left(rounds)
+
+    def down_copy(c, k):
+        return cross(dw_sum.at[c, k], dw_down.at[c, k], down_send.at[c, k], down_recv.at[c, k],
+                     group - 2)
+
+    def up_copy(c, k):
+        return cross(dw_sum.at[c, k], dw_up.at[c, k], up_send.at[c, k], up_recv.at[c, k], group + 2)
+
+    def move(j, k):
+        @pl.when(chip > j)
+        def _():
+            @pl.when(chip + 1 < chips)
+            def _():
+                down_copy(j, k).wait_recv()
+                both = dw_sum[j, k].astype(jnp.float32) + dw_down[j, k].astype(jnp.float32)
+                dw_sum[j, k] = both.astype(jnp.bfloat16)
+
+            down_copy(j, k).start()
+
+        c = chips - 1 - j
+
+        @pl.when(chip < c)
+        def _():
+            @pl.when(chip >= 1)
+            def _():
+                up_copy(c, k).wait_recv()
+                both = dw_sum[c, k].astype(jnp.float32) + dw_up[c, k].astype(jnp.float32)
+                dw_sum[c, k] = both.astype(jnp.bfloat16)
+
+            up_copy(c, k).start()
+
     gain_copies = [
         send(gg_ref, gain_one.at[me], gain_send.at[k], gain_recv.at[me], peer)
         for k, peer in enumerate(peers)
     ]
-    for copy in gain_copies:
-        copy.start()
-    for copy in pair_copies:
-        copy.wait()
-    for c in range(chips):
-        both = dw_part[c * 2 + core].astype(jnp.float32) + dw_pair[c].astype(jnp.float32)
-        dw_sum[c] = both.astype(jnp.bfloat16)
-
-    def down_copy(c, k):
-        return cross(dw_sum.at[c, k], dw_down.at[c, k], down_send.at[c, k], down_recv.at[c, k],
-                     group - 2)
-
-    def up_copy(c, k):
-        return cross(dw_sum.at[c, k], dw_up.at[c, k], up_send.at[c, k], up_recv.at[c, k], group + 2)
-
-    def move(j, k):
-        @pl.when(chip > j)
-        def _():
-            @pl.when(chip + 1 < chips)
-            def _():
-                down_copy(j, k).wait_recv()
-                both = dw_sum[j, k].astype(jnp.float32) + dw_down[j, k].astype(jnp.float32)
-                dw_sum[j, k] = both.astype(jnp.bfloat16)
-
-            down_copy(j, k).start()
-
-        c = chips - 1 - j
-
-        @pl.when(chip < c)
-        def _():
-            @pl.when(chip >= 1)
-            def _():
-                up_copy(c, k).wait_recv()
-                both = dw_sum[c, k].astype(jnp.float32) + dw_up[c, k].astype(jnp.float32)
-                dw_sum[c, k] = both.astype(jnp.bfloat16)
-
-            up_copy(c, k).start()
-
+    left = list(range(rounds + 2, rounds + 1 + chips))
     for j in range(chips - 1):
+        for c in (j, chips - 1 - j):
+            if c in ready:
+                ready.remove(c)
+                pair_copies[c].wait()
+                both = dw_part[c * 2 + core].astype(jnp.float32) + dw_pair[c].astype(jnp.float32)
+                dw_sum[c] = both.astype(jnp.bfloat16)
         for k in range(3):
             move(j, k)
-    for t in range(rounds + 2, rounds + 1 + chips):
+            if j == 0 and k == 0:
+                finish(rounds - 1)
+                relay_left(rounds + 1)
+                gain_one[me] = gg_ref[...]
+                for copy in gain_copies:
+                    copy.start()
+            elif j >= 1 and k != 1 and left:
+                relay_left(left.pop(0))
+    for t in left:
         relay_left(t)
     for peer in peers:
         send(gg_ref, gain_one.at[peer], gain_send.at[0], gain_recv.at[peer], peer).wait_recv()
@@ -444,6 +541,8 @@
         return carry
 
     lax.fori_loop(0, rounds, settle, 0)
+    for copy in far_pool + far_passed:
+        copy.wait_send()
 
     def place(t, carry):
         ig_ref[t] = (placed[source_ref[t]].astype(jnp.float32) * keep_ref[t]).astype(jnp.bfloat16)
@@ -500,7 +599,7 @@
     dma = pltpu.SemaphoreType.DMA
     bf16 = jnp.bfloat16
     return pl.pallas_call(
-        functools.partial(block_kernel, n, groups, rounds, 3),
+        functools.partial(block_kernel, n, groups, rounds, 2, min(early_round, rounds)),
         in_specs=[smem] * 4 + [vmem] * 6,
         out_specs=[vmem] * 5,
         out_shape=[
@@ -533,9 +632,14 @@
             pltpu.VMEM((chips, 3, block, inner), bf16),
             pltpu.VMEM((chips, 3, block, inner), bf16),
             pltpu.VMEM((2, max(slots - rounds, 1), rows, width), bf16),
+            pltpu.VMEM((2, max(2 * (slots - rounds), 1), rows, width), bf16),
             pltpu.SMEM((rounds,), jnp.float32),
             pltpu.SMEM((slots,), jnp.int32),
             pltpu.SMEM((slots,), jnp.float32),
+            pltpu.SMEM((rounds,), jnp.int32),
+            pltpu.SMEM((rounds,), jnp.int32),
+            pltpu.SMEM((rounds,), jnp.int32),
+            pltpu.SMEM((slots,), jnp.int32),
             dma((rounds, n + 2 * (high - 1))),
             dma((rounds, 2, n)),
             dma((rounds,)),
@@ -558,8 +662,8 @@
             dma((chips, 3)),
             dma((chips, 3)),
             dma((chips, 3)),
-            dma((2,)),
-            dma((2,)),
+            dma((2, 3)),
+            dma((2, 3)),
         ],
         compiler_params=pltpu.CompilerParams(
             collective_id=ident, has_side_effects=True, vmem_limit_bytes=60 * 1024 * 1024
@@ -584,12 +688,39 @@
     )(ig, gg, dv, dg, do)
 
 
+def choose_kernel(plans, groups, slots, steps_ref, choice_ref):
+    choice = jnp.int32(0)
+    blocked = jnp.int32(1)
+    for rounds in plans[:-1]:
+        lacking = jnp.int32(0)
+        for base in range(0, groups, 4):
+            lives = [jnp.clip(steps_ref[base + q] - 29, 1, slots) for q in range(4)]
+            _, _, _, spare_at, free_at = share(lives, rounds, min(early_round, rounds))
+            lacking = jnp.maximum(lacking, spare_at[4] - free_at[4])
+        blocked = jnp.where(lacking > 0, blocked, 0)
+        choice = choice + blocked
+    choice_ref[0] = choice
+
+
+def choose(plans, groups, slots, steps):
+    smem = pl.BlockSpec(memory_space=pltpu.SMEM)
+    return pl.pallas_call(
+        functools.partial(choose_kernel, plans, groups, slots), in_specs=[smem], out_specs=smem,
+        out_shape=jax.ShapeDtypeStruct((1,), jnp.int32),
+    )(steps)[0]
+
+
 def per_device(latents, cotangent, trunc_steps, timesteps, tile_map, gain, w_value, w_gate, w_out):
     slots = latents.shape[0]
     n, groups = lax.axis_size("tensor"), lax.axis_size("dp")
     table = jnp.asarray(noise_table())
     args = (trunc_steps, timesteps, tile_map, table, latents, cotangent, gain, w_value, w_gate, w_out)
-    results = block_backward(n, groups, slots, 0, *args)
+    plans = [r for r in (6, 7, 8) if r < slots] + [slots]
+    choice = choose(plans, groups, slots, trunc_steps)
+    results = lax.switch(
+        choice, [functools.partial(block_backward, n, groups, r, k) for k, r in enumerate(plans)],
+        *args,
+    )
     return tuple(emit(*results))
 
 

time: 159 us -> 126 us (0.79)
  Pallas kernels: 157 us -> 122 us
    pallas_call x1 -> x2, Pallas kernels: 155 us -> 121 us  [the longest x1 119 us: block_backward(): pl.pallas_call(functools.partial(block_kernel, n, groups, rounds, 2, min(...]
where the time goes in v2:
time: 126 us; the launch traced here: 125 us
  Pallas kernels  122 us (97%)
  local copies, waits for them, and re-layouts  1.35 us (1%)
  between operations  1.34 us (1%)
    pallas_call x1, Pallas kernels, block_backward(): pl.pallas_call(functools.partial(block_kernel, n, groups, rounds, 2, min(...  119 us

profile of v2, /device:TPU:12, one launch (start us, length us, event | category | flops | bytes accessed | tf_op | source)
XLA Modules:
  0.0 125.0 jit_solution(15914097296093798549)
XLA Ops:
  0.6 0.0 copy-start
  0.6 1.5 %shard_map.137 = s32[1]{0:T(128)} custom-call(s32[8]{0:T(128)} %steps_ref.1), custom_call_target="tpu_custom_call" | custom-call | tf_op jit(solution)/shard_map/pallas_call | solution.py:707
  2.8 0.0 copy-start.5
  2.8 0.0 copy-start.6
  2.8 0.0 copy-start.7
  2.8 0.0 copy-done
  2.8 0.6 copy-done.5
  3.4 0.0 copy-done.6
  3.4 0.0 copy-done.7
  3.4 120.3 %conditional.1 = ((bf16[11,64,640]{2,1,0:T(8,128)(2,1)S(1)}, f32[1,640]{1,0:T(1,128)S(1)}, f32[80,640]{1,0:T(8,128)S(1)}, f32[80,640]{1,0:T(8,128)S(1)}, f32[80,640]{1,0:T(8,128)S(1)})) conditional(s32[]{:T(128)} %bitcast, (s32[8]{0:T(128)S(1)}, s32[88]{0:T(128)S(1)}, s32[88]{0:T(128)S(1)}, f32[1000]{0:T(1024)}, ...), branch_computations={%region_0.0_spmd, %region_1.0_spmd, %region_2.0_spmd, %region_3.0_... | conditional | bytes 16036 | solution.py:720
  3.4 0.0 copy-start.2
  3.4 0.7 copy-done.2
  4.1 119.1 %branch_1_fun.1 = (bf16[11,64,640]{2,1,0:T(8,128)(2,1)S(1)}, f32[1,640]{1,0:T(1,128)S(1)}, f32[80,640]{1,0:T(8,128)S(1)}, f32[80,640]{1,0:T(8,128)S(1)}, f32[80,640]{1,0:T(8,128)S(1)}) custom-call(s32[8]{0:T(128)S(1)} %get-tuple-element.90.steps_ref, s32[88]{0:T(128)S(1)} %get-tuple-element.91.times_ref, s32[88]{0:T(128)S(1)} %get-tuple-element.92.map_ref, ...), custom_call_target="tpu_custom_call" | custom-call | tf_op jit(solution)/shard_map/cond/branch_1_fun/pallas_call | solution.py:601
  123.8 1.2 shard_map.138
Async XLA Ops:
  0.6 2.2 %copy-start = (f32[640]{0:T(1024)S(1)}, f32[640]{0:T(1024)}, u32[]{:S(2)}) copy-start(f32[640]{0:T(1024)} %param.19) | copy-start | bytes 7684
  2.8 0.7 copy-start.5
  2.8 0.7 copy-start.6
  2.8 0.7 copy-start.7
  3.4 0.7 copy-start.2
